TPU v7x, 32 devices: a whole 2x2x4 slice. The times are simulated.
32 devices in a mesh: row: 8 (over z, y), col: 4 (over x, core).
Axes of the slice: x: 2, y: 2, z: 4, core: 2. Of those that a mesh axis runs over, the one named last changes fastest.
Arguments:
- rhs: float32 [2, 8, 64, 512], P(None, 'row'), may hold values from -6 to 6
- inverse_t: float32 [2, 8, 512, 512], P(None, 'row', None, 'col'), may hold values from -1 to 2, as said below
- u_factors: bfloat16 [2, 8, 4, 4, 32, 512], P(None, 'row', None, 'col'), may hold values from -0.14941406 to 0.14941406
- v_factors: bfloat16 [2, 8, 4, 4, 32, 512], P(None, 'row', None, 'col'), may hold values from -0.14941406 to 0.14941406
- tile_ranks: int32 [2, 8, 4, 4], P(None, 'row', None, 'col'), may hold values from 8 to 32
Outputs:
- solved: float32 [2, 8, 64, 512], P(None, 'row')
Inputs may be any that keep to these rules, and one draw needn't show every extreme that they name: `inverse_t`: each transposed inverse is nonsingular and of order one.
All inputs are finite; a program needn't handle non-finite values.
Results may differ from a plain program's by a relative error of at most 0.004.
Values may be sent and summed in bfloat16 or wider, within the bound.
No kernel may reach another device: no remote copies, remote signals or barrier semaphores. Data moves between devices by JAX's collectives and lax.ppermute only.
A program may use at most 64 MiB of HBM per device.

v0:
```python
import jax
import jax.numpy as jnp
from jax import lax
from jax.sharding import PartitionSpec as P


def broadcast(block, axis, source):
    block = jnp.where(lax.axis_index(axis) == source, block, jnp.zeros_like(block))
    return lax.psum(block, axis)


def pick(array, index, axis):
    return lax.dynamic_index_in_dim(array, index, axis, keepdims=False)


def on_device(rhs, inverse_t, u_factors, v_factors, tile_ranks):
    rhs_here = rhs[:, 0]
    slots = rhs_here.shape[0]
    rank_width = u_factors.shape[4]
    n_row = lax.axis_size("row")
    n_col = lax.axis_size("col")
    blocks = slots * n_row
    my_row = lax.axis_index("row")
    my_col = lax.axis_index("col")
    global_rows = jnp.arange(slots, dtype=jnp.int32) * n_row + my_row
    rank_cols = lax.broadcasted_iota(jnp.int32, (1, 1, rank_width), 2)
    start = jnp.zeros(rhs_here.shape, jnp.float32)

    def apply_update(totals, full, u_col, v_col, ranks, active):
        seg_b = full.astype(jnp.bfloat16)
        proj = jnp.einsum("rb,akb->ark", seg_b, v_col, preferred_element_type=jnp.float32)
        keep = (rank_cols < ranks[:, None, None]) & active[:, None, None]
        proj_b = jnp.where(keep, proj, 0.0).astype(jnp.bfloat16)
        update = jnp.einsum("ark,akb->arb", proj_b, u_col, preferred_element_type=jnp.float32)
        return totals + update

    inverse_here = inverse_t[:, 0]
    u_here = u_factors[:, 0, :, 0]
    v_here = v_factors[:, 0, :, 0]
    ranks_here = tile_ranks[:, 0, :, 0]

    def step(k, carry):
        totals, solved = carry
        k_slot = k // n_row
        k_row = k % n_row
        c_slot = k // n_col
        c_dev = k % n_col
        summed = lax.psum(pick(totals, k_slot, 0).astype(jnp.bfloat16), "col").astype(jnp.float32)
        segment = pick(rhs_here, k_slot, 0) - summed
        piece = jnp.dot(
            segment,
            pick(inverse_here, k_slot, 0),
            precision=lax.Precision.HIGHEST,
            preferred_element_type=jnp.float32,
        )
        spread = broadcast(piece, "row", k_row)
        full = lax.all_gather(spread, "col", axis=1, tiled=True)
        previous = pick(solved, k_slot, 0)
        solved = lax.dynamic_update_index_in_dim(
            solved, jnp.where(my_row == k_row, full, previous), k_slot, 0
        )
        u_col = pick(u_here, c_slot, 1)
        v_col = pick(v_here, c_slot, 1)
        ranks = pick(ranks_here, c_slot, 1)
        active = (global_rows > k) & (my_col == c_dev)
        totals = apply_update(totals, full, u_col, v_col, ranks, active)
        return (totals, solved)

    totals, solved = lax.fori_loop(0, blocks, step, (start, start))
    return solved[:, None]


def solution(mesh):
    in_specs = (
        P(None, "row", None, None),
        P(None, "row", None, "col"),
        P(None, "row", None, "col", None, None),
        P(None, "row", None, "col", None, None),
        P(None, "row", None, "col"),
    )
    out_specs = P(None, "row", None, None)
    return jax.shard_map(
        on_device, mesh=mesh, in_specs=in_specs, out_specs=out_specs, check_vma=False
    )
```

profile of v0, /device:TPU:0, one launch (start us, length us, event | category | flops | bytes accessed | tf_op | source)
XLA Modules:
  0.0 1234.3 jit_solution(4183829090954470033)
XLA Ops:
  9.3 1217.8 %while.21 = (s32[]{:T(128)}, f32[2,64,512]{2,1,0:T(8,128)S(1)}, f32[2,64,512]{2,1,0:T(8,128)S(1)}, s32[2,4]{0,1:T(4,128)S(1)}, s32[]{:T(128)}, /*index=5*/bf16[2...) while((s32[]{:T(128)}, f32[2,64,512]{2,1,0:T(8,128)S(1)}, ...), condition=%wide.region_3.4_spmd.clone.clone.clone, body=%wide.region_0.3_spmd.clone.clone.clone.sunk | while | flops 59039912 | bytes 3215025 | solution.py:69
  10.2 36.5 %all-reduce.2.cloned.1.call-done = bf16[64,512]{1,0:T(8,128)(2,1)} async-done(((bf16[64,512]{1,0:T(8,128)(2,1)}), bf16[64,512]{1,0:T(8,128)(2,1)}) %all-reduce.2.cloned.1.call-update) | async-done | bytes 65552 | tf_op jit(solution)/shard_map/while/body/eval_jaxpr/psum | solution.py:48
  47.8 37.1 %psum.39 = f32[64,128]{1,0:T(8,128)S(1)} all-reduce(f32[64,128]{1,0:T(8,128)S(1)} %convolution_select_fusion.3), channel_id=1, replica_groups=mesh['row'=8,'col'=4] {'row'}, use_global_device_ids=true, to_apply=%region_2.2 | all-reduce | flops 8192 | bytes 65536 | tf_op jit(solution)/shard_map/while/body/eval_jaxpr/psum | solution.py:9
  92.5 30.0 %all-reduce.2.cloned.1.call-done = bf16[64,512]{1,0:T(8,128)(2,1)} async-done(((bf16[64,512]{1,0:T(8,128)(2,1)}), bf16[64,512]{1,0:T(8,128)(2,1)}) %all-reduce.2.cloned.1.call-update) | async-done | bytes 65552 | tf_op jit(solution)/shard_map/while/body/eval_jaxpr/psum | solution.py:48
  123.7 37.1 %psum.39 = f32[64,128]{1,0:T(8,128)S(1)} all-reduce(f32[64,128]{1,0:T(8,128)S(1)} %convolution_select_fusion.3), channel_id=1, replica_groups=mesh['row'=8,'col'=4] {'row'}, use_global_device_ids=true, to_apply=%region_2.2 | all-reduce | flops 8192 | bytes 65536 | tf_op jit(solution)/shard_map/while/body/eval_jaxpr/psum | solution.py:9
  168.4 30.0 %all-reduce.2.cloned.1.call-done = bf16[64,512]{1,0:T(8,128)(2,1)} async-done(((bf16[64,512]{1,0:T(8,128)(2,1)}), bf16[64,512]{1,0:T(8,128)(2,1)}) %all-reduce.2.cloned.1.call-update) | async-done | bytes 65552 | tf_op jit(solution)/shard_map/while/body/eval_jaxpr/psum | solution.py:48
  199.5 37.1 %psum.39 = f32[64,128]{1,0:T(8,128)S(1)} all-reduce(f32[64,128]{1,0:T(8,128)S(1)} %convolution_select_fusion.3), channel_id=1, replica_groups=mesh['row'=8,'col'=4] {'row'}, use_global_device_ids=true, to_apply=%region_2.2 | all-reduce | flops 8192 | bytes 65536 | tf_op jit(solution)/shard_map/while/body/eval_jaxpr/psum | solution.py:9
  275.1 37.1 %psum.39 = f32[64,128]{1,0:T(8,128)S(1)} all-reduce(f32[64,128]{1,0:T(8,128)S(1)} %convolution_select_fusion.3), channel_id=1, replica_groups=mesh['row'=8,'col'=4] {'row'}, use_global_device_ids=true, to_apply=%region_2.2 | all-reduce | flops 8192 | bytes 65536 | tf_op jit(solution)/shard_map/while/body/eval_jaxpr/psum | solution.py:9
  350.6 37.1 %psum.39 = f32[64,128]{1,0:T(8,128)S(1)} all-reduce(f32[64,128]{1,0:T(8,128)S(1)} %convolution_select_fusion.3), channel_id=1, replica_groups=mesh['row'=8,'col'=4] {'row'}, use_global_device_ids=true, to_apply=%region_2.2 | all-reduce | flops 8192 | bytes 65536 | tf_op jit(solution)/shard_map/while/body/eval_jaxpr/psum | solution.py:9
  426.2 37.1 %psum.39 = f32[64,128]{1,0:T(8,128)S(1)} all-reduce(f32[64,128]{1,0:T(8,128)S(1)} %convolution_select_fusion.3), channel_id=1, replica_groups=mesh['row'=8,'col'=4] {'row'}, use_global_device_ids=true, to_apply=%region_2.2 | all-reduce | flops 8192 | bytes 65536 | tf_op jit(solution)/shard_map/while/body/eval_jaxpr/psum | solution.py:9
  470.9 30.0 %all-reduce.2.cloned.1.call-done = bf16[64,512]{1,0:T(8,128)(2,1)} async-done(((bf16[64,512]{1,0:T(8,128)(2,1)}), bf16[64,512]{1,0:T(8,128)(2,1)}) %all-reduce.2.cloned.1.call-update) | async-done | bytes 65552 | tf_op jit(solution)/shard_map/while/body/eval_jaxpr/psum | solution.py:48
  502.1 37.1 %psum.39 = f32[64,128]{1,0:T(8,128)S(1)} all-reduce(f32[64,128]{1,0:T(8,128)S(1)} %convolution_select_fusion.3), channel_id=1, replica_groups=mesh['row'=8,'col'=4] {'row'}, use_global_device_ids=true, to_apply=%region_2.2 | all-reduce | flops 8192 | bytes 65536 | tf_op jit(solution)/shard_map/while/body/eval_jaxpr/psum | solution.py:9
  546.8 30.0 %all-reduce.2.cloned.1.call-done = bf16[64,512]{1,0:T(8,128)(2,1)} async-done(((bf16[64,512]{1,0:T(8,128)(2,1)}), bf16[64,512]{1,0:T(8,128)(2,1)}) %all-reduce.2.cloned.1.call-update) | async-done | bytes 65552 | tf_op jit(solution)/shard_map/while/body/eval_jaxpr/psum | solution.py:48
  577.9 37.1 %psum.39 = f32[64,128]{1,0:T(8,128)S(1)} all-reduce(f32[64,128]{1,0:T(8,128)S(1)} %convolution_select_fusion.3), channel_id=1, replica_groups=mesh['row'=8,'col'=4] {'row'}, use_global_device_ids=true, to_apply=%region_2.2 | all-reduce | flops 8192 | bytes 65536 | tf_op jit(solution)/shard_map/while/body/eval_jaxpr/psum | solution.py:9
  622.6 30.0 %all-reduce.2.cloned.1.call-done = bf16[64,512]{1,0:T(8,128)(2,1)} async-done(((bf16[64,512]{1,0:T(8,128)(2,1)}), bf16[64,512]{1,0:T(8,128)(2,1)}) %all-reduce.2.cloned.1.call-update) | async-done | bytes 65552 | tf_op jit(solution)/shard_map/while/body/eval_jaxpr/psum | solution.py:48
  653.8 37.1 %psum.39 = f32[64,128]{1,0:T(8,128)S(1)} all-reduce(f32[64,128]{1,0:T(8,128)S(1)} %convolution_select_fusion.3), channel_id=1, replica_groups=mesh['row'=8,'col'=4] {'row'}, use_global_device_ids=true, to_apply=%region_2.2 | all-reduce | flops 8192 | bytes 65536 | tf_op jit(solution)/shard_map/while/body/eval_jaxpr/psum | solution.py:9
  729.4 37.1 %psum.39 = f32[64,128]{1,0:T(8,128)S(1)} all-reduce(f32[64,128]{1,0:T(8,128)S(1)} %convolution_select_fusion.3), channel_id=1, replica_groups=mesh['row'=8,'col'=4] {'row'}, use_global_device_ids=true, to_apply=%region_2.2 | all-reduce | flops 8192 | bytes 65536 | tf_op jit(solution)/shard_map/while/body/eval_jaxpr/psum | solution.py:9
  805.2 37.1 %psum.39 = f32[64,128]{1,0:T(8,128)S(1)} all-reduce(f32[64,128]{1,0:T(8,128)S(1)} %convolution_select_fusion.3), channel_id=1, replica_groups=mesh['row'=8,'col'=4] {'row'}, use_global_device_ids=true, to_apply=%region_2.2 | all-reduce | flops 8192 | bytes 65536 | tf_op jit(solution)/shard_map/while/body/eval_jaxpr/psum | solution.py:9
  880.8 37.1 %psum.39 = f32[64,128]{1,0:T(8,128)S(1)} all-reduce(f32[64,128]{1,0:T(8,128)S(1)} %convolution_select_fusion.3), channel_id=1, replica_groups=mesh['row'=8,'col'=4] {'row'}, use_global_device_ids=true, to_apply=%region_2.2 | all-reduce | flops 8192 | bytes 65536 | tf_op jit(solution)/shard_map/while/body/eval_jaxpr/psum | solution.py:9
  925.5 30.0 %all-reduce.2.cloned.1.call-done = bf16[64,512]{1,0:T(8,128)(2,1)} async-done(((bf16[64,512]{1,0:T(8,128)(2,1)}), bf16[64,512]{1,0:T(8,128)(2,1)}) %all-reduce.2.cloned.1.call-update) | async-done | bytes 65552 | tf_op jit(solution)/shard_map/while/body/eval_jaxpr/psum | solution.py:48
  956.6 37.1 %psum.39 = f32[64,128]{1,0:T(8,128)S(1)} all-reduce(f32[64,128]{1,0:T(8,128)S(1)} %convolution_select_fusion.3), channel_id=1, replica_groups=mesh['row'=8,'col'=4] {'row'}, use_global_device_ids=true, to_apply=%region_2.2 | all-reduce | flops 8192 | bytes 65536 | tf_op jit(solution)/shard_map/while/body/eval_jaxpr/psum | solution.py:9
  1032.2 37.1 %psum.39 = f32[64,128]{1,0:T(8,128)S(1)} all-reduce(f32[64,128]{1,0:T(8,128)S(1)} %convolution_select_fusion.3), channel_id=1, replica_groups=mesh['row'=8,'col'=4] {'row'}, use_global_device_ids=true, to_apply=%region_2.2 | all-reduce | flops 8192 | bytes 65536 | tf_op jit(solution)/shard_map/while/body/eval_jaxpr/psum | solution.py:9
  1107.7 37.1 %psum.39 = f32[64,128]{1,0:T(8,128)S(1)} all-reduce(f32[64,128]{1,0:T(8,128)S(1)} %convolution_select_fusion.3), channel_id=1, replica_groups=mesh['row'=8,'col'=4] {'row'}, use_global_device_ids=true, to_apply=%region_2.2 | all-reduce | flops 8192 | bytes 65536 | tf_op jit(solution)/shard_map/while/body/eval_jaxpr/psum | solution.py:9
  1183.3 37.1 %psum.39 = f32[64,128]{1,0:T(8,128)S(1)} all-reduce(f32[64,128]{1,0:T(8,128)S(1)} %convolution_select_fusion.3), channel_id=1, replica_groups=mesh['row'=8,'col'=4] {'row'}, use_global_device_ids=true, to_apply=%region_2.2 | all-reduce | flops 8192 | bytes 65536 | tf_op jit(solution)/shard_map/while/body/eval_jaxpr/psum | solution.py:9
  (211 shorter events, 409.0 us)
Async XLA Ops:
  6.5 1.8 copy-start
  8.3 1.0 copy-start.2
  9.3 37.4 %all-reduce.2.cloned.1.call-start = ((), (), s32[]{:S(2)}) async-start(), calls=%async_computation | async-start | bytes 131072 | tf_op jit(solution)/shard_map/while/body/eval_jaxpr/psum | solution.py:48
  91.6 30.9 %all-reduce.2.cloned.1.call-start = ((), (), s32[]{:S(2)}) async-start(), calls=%async_computation | async-start | bytes 131072 | tf_op jit(solution)/shard_map/while/body/eval_jaxpr/psum | solution.py:48
  167.5 30.9 %all-reduce.2.cloned.1.call-start = ((), (), s32[]{:S(2)}) async-start(), calls=%async_computation | async-start | bytes 131072 | tf_op jit(solution)/shard_map/while/body/eval_jaxpr/psum | solution.py:48
  243.3 30.6 %all-reduce.2.cloned.1.call-start = ((), (), s32[]{:S(2)}) async-start(), calls=%async_computation | async-start | bytes 131072 | tf_op jit(solution)/shard_map/while/body/eval_jaxpr/psum | solution.py:48
  318.9 30.6 %all-reduce.2.cloned.1.call-start = ((), (), s32[]{:S(2)}) async-start(), calls=%async_computation | async-start | bytes 131072 | tf_op jit(solution)/shard_map/while/body/eval_jaxpr/psum | solution.py:48
  394.4 30.6 %all-reduce.2.cloned.1.call-start = ((), (), s32[]{:S(2)}) async-start(), calls=%async_computation | async-start | bytes 131072 | tf_op jit(solution)/shard_map/while/body/eval_jaxpr/psum | solution.py:48
  470.0 30.9 %all-reduce.2.cloned.1.call-start = ((), (), s32[]{:S(2)}) async-start(), calls=%async_computation | async-start | bytes 131072 | tf_op jit(solution)/shard_map/while/body/eval_jaxpr/psum | solution.py:48
  545.8 30.9 %all-reduce.2.cloned.1.call-start = ((), (), s32[]{:S(2)}) async-start(), calls=%async_computation | async-start | bytes 131072 | tf_op jit(solution)/shard_map/while/body/eval_jaxpr/psum | solution.py:48
  621.7 30.9 %all-reduce.2.cloned.1.call-start = ((), (), s32[]{:S(2)}) async-start(), calls=%async_computation | async-start | bytes 131072 | tf_op jit(solution)/shard_map/while/body/eval_jaxpr/psum | solution.py:48
  697.6 30.6 %all-reduce.2.cloned.1.call-start = ((), (), s32[]{:S(2)}) async-start(), calls=%async_computation | async-start | bytes 131072 | tf_op jit(solution)/shard_map/while/body/eval_jaxpr/psum | solution.py:48
  773.1 30.9 %all-reduce.2.cloned.1.call-start = ((), (), s32[]{:S(2)}) async-start(), calls=%async_computation | async-start | bytes 131072 | tf_op jit(solution)/shard_map/while/body/eval_jaxpr/psum | solution.py:48
  849.0 30.6 %all-reduce.2.cloned.1.call-start = ((), (), s32[]{:S(2)}) async-start(), calls=%async_computation | async-start | bytes 131072 | tf_op jit(solution)/shard_map/while/body/eval_jaxpr/psum | solution.py:48
  924.6 30.9 %all-reduce.2.cloned.1.call-start = ((), (), s32[]{:S(2)}) async-start(), calls=%async_computation | async-start | bytes 131072 | tf_op jit(solution)/shard_map/while/body/eval_jaxpr/psum | solution.py:48
  1000.4 30.6 %all-reduce.2.cloned.1.call-start = ((), (), s32[]{:S(2)}) async-start(), calls=%async_computation | async-start | bytes 131072 | tf_op jit(solution)/shard_map/while/body/eval_jaxpr/psum | solution.py:48
  1076.0 30.6 %all-reduce.2.cloned.1.call-start = ((), (), s32[]{:S(2)}) async-start(), calls=%async_computation | async-start | bytes 131072 | tf_op jit(solution)/shard_map/while/body/eval_jaxpr/psum | solution.py:48
  1151.5 30.6 %all-reduce.2.cloned.1.call-start = ((), (), s32[]{:S(2)}) async-start(), calls=%async_computation | async-start | bytes 131072 | tf_op jit(solution)/shard_map/while/body/eval_jaxpr/psum | solution.py:48
  1227.1 0.7 copy-start.1
Sparse Core Ops, SparseCore 0:
  12.4 34.2 all-reduce.1
  94.7 27.7 all-reduce.1
  170.6 27.7 all-reduce.1
  246.1 27.7 all-reduce.1
  321.7 27.7 all-reduce.1
  397.2 27.7 all-reduce.1
  473.1 27.7 all-reduce.1
  549.0 27.7 all-reduce.1
  624.8 27.7 all-reduce.1
  700.4 27.7 all-reduce.1
  776.3 27.7 all-reduce.1
  851.8 27.7 all-reduce.1
  927.7 27.7 all-reduce.1
  1003.2 27.7 all-reduce.1
  1078.8 27.7 all-reduce.1
  1154.3 27.7 all-reduce.1
where the time goes:
time: 1240 us; the launch traced here: 1230 us
  blocking collectives  680 us (55%)
  waiting for transfers between devices  484 us (39%)
  matrix products  38 us (3%)
  local copies, waits for them, and re-layouts  14 us (1%)
  between operations  13.1 us (1%)
    psum x16, blocking collectives, broadcast(): return lax.psum(block, axis)  593 us
    psum x16, waiting for transfers between devices, step(): lax.psum(pick(totals, k_slot, 0).astype(jnp.bfloat16), 'col')  484 us
    all_gather x16, blocking collectives, step(): full = lax.all_gather(spread, 'col', axis=1, tiled=True)  86.4 us
  transfers between devices with their start and end apart: 16, of which 16 were waited for; matrix products, arithmetic and copies ran while one was open for 0% of the time, Pallas kernels for 0%

commit v1 on v0

--- a/solution.py
+++ b/solution.py
@@ -6,7 +6,7 @@
 
 def broadcast(block, axis, source):
     block = jnp.where(lax.axis_index(axis) == source, block, jnp.zeros_like(block))
-    return lax.psum(block, axis)
+    return jnp.sum(lax.all_gather(block, axis), axis=0)
 
 
 def pick(array, index, axis):

time: 1240 us -> 1190 us (0.960)
  blocking collectives: 680 us -> 582 us
  waiting for transfers between devices: 484 us -> 539 us
    psum x16 -> x0, blocking collectives: 593 us -> none  [broadcast(): return lax.psum(block, axis)]
    all_gather x0 -> x16, blocking collectives: none -> 495 us  [broadcast(): return jnp.sum(lax.all_gather(block, axis), axis=0)]
    psum x16, waiting for transfers between devices: 484 us -> 539 us  [step(): lax.psum(pick(totals, k_slot, 0).astype(jnp.bfloat16), 'col')]
where the time goes in v1:
time: 1190 us
  blocking collectives  582 us (49%)
  waiting for transfers between devices  539 us (45%)
  matrix products  38 us (3%)
  local copies, waits for them, and re-layouts  14 us (1%)
  between operations  13.1 us (1%)
    psum x16, waiting for transfers between devices, step(): lax.psum(pick(totals, k_slot, 0).astype(jnp.bfloat16), 'col')  539 us
    all_gather x16, blocking collectives, broadcast(): return jnp.sum(lax.all_gather(block, axis), axis=0)  495 us
    all_gather x16, blocking collectives, step(): full = lax.all_gather(spread, 'col', axis=1, tiled=True)  86.7 us
  transfers between devices with their start and end apart: 16, of which 16 were waited for; matrix products, arithmetic and copies ran while one was open for 0% of the time, Pallas kernels for 0%

profile of v1, /device:TPU:0, one launch (start us, length us, event | category | flops | bytes accessed | tf_op | source)
XLA Modules:
  0.0 1190.7 jit_solution(5614252504671415684)
XLA Ops:
  9.3 1174.2 %while.21 = (s32[]{:T(128)}, f32[2,64,512]{2,1,0:T(8,128)S(1)}, f32[2,64,512]{2,1,0:T(8,128)S(1)}, s32[2,4]{0,1:T(4,128)S(1)}, s32[]{:T(128)}, /*index=5*/bf16[2...) while((s32[]{:T(128)}, f32[2,64,512]{2,1,0:T(8,128)S(1)}, ...), condition=%wide.region_3.4_spmd.clone.clone.clone, body=%wide.region_0.3_spmd.clone.clone.clone.sunk | while | flops 59089064 | bytes 3739325 | solution.py:69
  10.2 36.5 %all-reduce.2.cloned.1.call-done = bf16[64,512]{1,0:T(8,128)(2,1)} async-done(((bf16[64,512]{1,0:T(8,128)(2,1)}), bf16[64,512]{1,0:T(8,128)(2,1)}) %all-reduce.2.cloned.1.call-update) | async-done | bytes 65552 | tf_op jit(solution)/shard_map/while/body/eval_jaxpr/psum | solution.py:48
  86.4 33.7 %all-reduce.2.cloned.1.call-done = bf16[64,512]{1,0:T(8,128)(2,1)} async-done(((bf16[64,512]{1,0:T(8,128)(2,1)}), bf16[64,512]{1,0:T(8,128)(2,1)}) %all-reduce.2.cloned.1.call-update) | async-done | bytes 65552 | tf_op jit(solution)/shard_map/while/body/eval_jaxpr/psum | solution.py:48
  121.2 30.9 %all-gather.5 = f32[512,128]{1,0:T(8,128)S(1)} all-gather(f32[64,128]{1,0:T(8,128)S(1)} %convolution_select_fusion.3), channel_id=2, replica_groups=mesh['row'=8,'col'=4] {'row'}, dimensions={0}, use_global_device_ids=true | all-gather | bytes 294912 | tf_op jit(solution)/shard_map/while/body/eval_jaxpr/all_gather | solution.py:9
  159.8 33.6 %all-reduce.2.cloned.1.call-done = bf16[64,512]{1,0:T(8,128)(2,1)} async-done(((bf16[64,512]{1,0:T(8,128)(2,1)}), bf16[64,512]{1,0:T(8,128)(2,1)}) %all-reduce.2.cloned.1.call-update) | async-done | bytes 65552 | tf_op jit(solution)/shard_map/while/body/eval_jaxpr/psum | solution.py:48
  194.5 30.9 %all-gather.5 = f32[512,128]{1,0:T(8,128)S(1)} all-gather(f32[64,128]{1,0:T(8,128)S(1)} %convolution_select_fusion.3), channel_id=2, replica_groups=mesh['row'=8,'col'=4] {'row'}, dimensions={0}, use_global_device_ids=true | all-gather | bytes 294912 | tf_op jit(solution)/shard_map/while/body/eval_jaxpr/all_gather | solution.py:9
  233.1 33.3 %all-reduce.2.cloned.1.call-done = bf16[64,512]{1,0:T(8,128)(2,1)} async-done(((bf16[64,512]{1,0:T(8,128)(2,1)}), bf16[64,512]{1,0:T(8,128)(2,1)}) %all-reduce.2.cloned.1.call-update) | async-done | bytes 65552 | tf_op jit(solution)/shard_map/while/body/eval_jaxpr/psum | solution.py:48
  267.6 30.9 %all-gather.5 = f32[512,128]{1,0:T(8,128)S(1)} all-gather(f32[64,128]{1,0:T(8,128)S(1)} %convolution_select_fusion.3), channel_id=2, replica_groups=mesh['row'=8,'col'=4] {'row'}, dimensions={0}, use_global_device_ids=true | all-gather | bytes 294912 | tf_op jit(solution)/shard_map/while/body/eval_jaxpr/all_gather | solution.py:9
  306.2 33.3 %all-reduce.2.cloned.1.call-done = bf16[64,512]{1,0:T(8,128)(2,1)} async-done(((bf16[64,512]{1,0:T(8,128)(2,1)}), bf16[64,512]{1,0:T(8,128)(2,1)}) %all-reduce.2.cloned.1.call-update) | async-done | bytes 65552 | tf_op jit(solution)/shard_map/while/body/eval_jaxpr/psum | solution.py:48
  340.6 30.9 %all-gather.5 = f32[512,128]{1,0:T(8,128)S(1)} all-gather(f32[64,128]{1,0:T(8,128)S(1)} %convolution_select_fusion.3), channel_id=2, replica_groups=mesh['row'=8,'col'=4] {'row'}, dimensions={0}, use_global_device_ids=true | all-gather | bytes 294912 | tf_op jit(solution)/shard_map/while/body/eval_jaxpr/all_gather | solution.py:9
  379.2 33.3 %all-reduce.2.cloned.1.call-done = bf16[64,512]{1,0:T(8,128)(2,1)} async-done(((bf16[64,512]{1,0:T(8,128)(2,1)}), bf16[64,512]{1,0:T(8,128)(2,1)}) %all-reduce.2.cloned.1.call-update) | async-done | bytes 65552 | tf_op jit(solution)/shard_map/while/body/eval_jaxpr/psum | solution.py:48
  452.3 33.7 %all-reduce.2.cloned.1.call-done = bf16[64,512]{1,0:T(8,128)(2,1)} async-done(((bf16[64,512]{1,0:T(8,128)(2,1)}), bf16[64,512]{1,0:T(8,128)(2,1)}) %all-reduce.2.cloned.1.call-update) | async-done | bytes 65552 | tf_op jit(solution)/shard_map/while/body/eval_jaxpr/psum | solution.py:48
  487.1 30.9 %all-gather.5 = f32[512,128]{1,0:T(8,128)S(1)} all-gather(f32[64,128]{1,0:T(8,128)S(1)} %convolution_select_fusion.3), channel_id=2, replica_groups=mesh['row'=8,'col'=4] {'row'}, dimensions={0}, use_global_device_ids=true | all-gather | bytes 294912 | tf_op jit(solution)/shard_map/while/body/eval_jaxpr/all_gather | solution.py:9
  525.7 33.7 %all-reduce.2.cloned.1.call-done = bf16[64,512]{1,0:T(8,128)(2,1)} async-done(((bf16[64,512]{1,0:T(8,128)(2,1)}), bf16[64,512]{1,0:T(8,128)(2,1)}) %all-reduce.2.cloned.1.call-update) | async-done | bytes 65552 | tf_op jit(solution)/shard_map/while/body/eval_jaxpr/psum | solution.py:48
  560.4 30.9 %all-gather.5 = f32[512,128]{1,0:T(8,128)S(1)} all-gather(f32[64,128]{1,0:T(8,128)S(1)} %convolution_select_fusion.3), channel_id=2, replica_groups=mesh['row'=8,'col'=4] {'row'}, dimensions={0}, use_global_device_ids=true | all-gather | bytes 294912 | tf_op jit(solution)/shard_map/while/body/eval_jaxpr/all_gather | solution.py:9
  599.0 33.7 %all-reduce.2.cloned.1.call-done = bf16[64,512]{1,0:T(8,128)(2,1)} async-done(((bf16[64,512]{1,0:T(8,128)(2,1)}), bf16[64,512]{1,0:T(8,128)(2,1)}) %all-reduce.2.cloned.1.call-update) | async-done | bytes 65552 | tf_op jit(solution)/shard_map/while/body/eval_jaxpr/psum | solution.py:48
  672.4 33.3 %all-reduce.2.cloned.1.call-done = bf16[64,512]{1,0:T(8,128)(2,1)} async-done(((bf16[64,512]{1,0:T(8,128)(2,1)}), bf16[64,512]{1,0:T(8,128)(2,1)}) %all-reduce.2.cloned.1.call-update) | async-done | bytes 65552 | tf_op jit(solution)/shard_map/while/body/eval_jaxpr/psum | solution.py:48
  745.5 33.7 %all-reduce.2.cloned.1.call-done = bf16[64,512]{1,0:T(8,128)(2,1)} async-done(((bf16[64,512]{1,0:T(8,128)(2,1)}), bf16[64,512]{1,0:T(8,128)(2,1)}) %all-reduce.2.cloned.1.call-update) | async-done | bytes 65552 | tf_op jit(solution)/shard_map/while/body/eval_jaxpr/psum | solution.py:48
  818.9 33.3 %all-reduce.2.cloned.1.call-done = bf16[64,512]{1,0:T(8,128)(2,1)} async-done(((bf16[64,512]{1,0:T(8,128)(2,1)}), bf16[64,512]{1,0:T(8,128)(2,1)}) %all-reduce.2.cloned.1.call-update) | async-done | bytes 65552 | tf_op jit(solution)/shard_map/while/body/eval_jaxpr/psum | solution.py:48
  891.9 33.7 %all-reduce.2.cloned.1.call-done = bf16[64,512]{1,0:T(8,128)(2,1)} async-done(((bf16[64,512]{1,0:T(8,128)(2,1)}), bf16[64,512]{1,0:T(8,128)(2,1)}) %all-reduce.2.cloned.1.call-update) | async-done | bytes 65552 | tf_op jit(solution)/shard_map/while/body/eval_jaxpr/psum | solution.py:48
  965.3 33.3 %all-reduce.2.cloned.1.call-done = bf16[64,512]{1,0:T(8,128)(2,1)} async-done(((bf16[64,512]{1,0:T(8,128)(2,1)}), bf16[64,512]{1,0:T(8,128)(2,1)}) %all-reduce.2.cloned.1.call-update) | async-done | bytes 65552 | tf_op jit(solution)/shard_map/while/body/eval_jaxpr/psum | solution.py:48
  999.8 30.9 %all-gather.5 = f32[512,128]{1,0:T(8,128)S(1)} all-gather(f32[64,128]{1,0:T(8,128)S(1)} %convolution_select_fusion.3), channel_id=2, replica_groups=mesh['row'=8,'col'=4] {'row'}, dimensions={0}, use_global_device_ids=true | all-gather | bytes 294912 | tf_op jit(solution)/shard_map/while/body/eval_jaxpr/all_gather | solution.py:9
  1038.3 33.3 %all-reduce.2.cloned.1.call-done = bf16[64,512]{1,0:T(8,128)(2,1)} async-done(((bf16[64,512]{1,0:T(8,128)(2,1)}), bf16[64,512]{1,0:T(8,128)(2,1)}) %all-reduce.2.cloned.1.call-update) | async-done | bytes 65552 | tf_op jit(solution)/shard_map/while/body/eval_jaxpr/psum | solution.py:48
  1111.4 33.3 %all-reduce.2.cloned.1.call-done = bf16[64,512]{1,0:T(8,128)(2,1)} async-done(((bf16[64,512]{1,0:T(8,128)(2,1)}), bf16[64,512]{1,0:T(8,128)(2,1)}) %all-reduce.2.cloned.1.call-update) | async-done | bytes 65552 | tf_op jit(solution)/shard_map/while/body/eval_jaxpr/psum | solution.py:48
  (227 shorter events, 420.3 us)
Async XLA Ops:
  6.5 1.8 copy-start
  8.3 1.0 copy-start.2
  9.3 37.4 %all-reduce.2.cloned.1.call-start = ((), (), s32[]{:S(2)}) async-start(), calls=%async_computation | async-start | bytes 131072 | tf_op jit(solution)/shard_map/while/body/eval_jaxpr/psum | solution.py:48
  85.5 34.6 %all-reduce.2.cloned.1.call-start = ((), (), s32[]{:S(2)}) async-start(), calls=%async_computation | async-start | bytes 131072 | tf_op jit(solution)/shard_map/while/body/eval_jaxpr/psum | solution.py:48
  158.8 34.6 %all-reduce.2.cloned.1.call-start = ((), (), s32[]{:S(2)}) async-start(), calls=%async_computation | async-start | bytes 131072 | tf_op jit(solution)/shard_map/while/body/eval_jaxpr/psum | solution.py:48
  232.2 34.2 %all-reduce.2.cloned.1.call-start = ((), (), s32[]{:S(2)}) async-start(), calls=%async_computation | async-start | bytes 131072 | tf_op jit(solution)/shard_map/while/body/eval_jaxpr/psum | solution.py:48
  305.2 34.3 %all-reduce.2.cloned.1.call-start = ((), (), s32[]{:S(2)}) async-start(), calls=%async_computation | async-start | bytes 131072 | tf_op jit(solution)/shard_map/while/body/eval_jaxpr/psum | solution.py:48
  378.3 34.2 %all-reduce.2.cloned.1.call-start = ((), (), s32[]{:S(2)}) async-start(), calls=%async_computation | async-start | bytes 131072 | tf_op jit(solution)/shard_map/while/body/eval_jaxpr/psum | solution.py:48
  451.3 34.6 %all-reduce.2.cloned.1.call-start = ((), (), s32[]{:S(2)}) async-start(), calls=%async_computation | async-start | bytes 131072 | tf_op jit(solution)/shard_map/while/body/eval_jaxpr/psum | solution.py:48
  524.7 34.6 %all-reduce.2.cloned.1.call-start = ((), (), s32[]{:S(2)}) async-start(), calls=%async_computation | async-start | bytes 131072 | tf_op jit(solution)/shard_map/while/body/eval_jaxpr/psum | solution.py:48
  598.1 34.6 %all-reduce.2.cloned.1.call-start = ((), (), s32[]{:S(2)}) async-start(), calls=%async_computation | async-start | bytes 131072 | tf_op jit(solution)/shard_map/while/body/eval_jaxpr/psum | solution.py:48
  671.5 34.3 %all-reduce.2.cloned.1.call-start = ((), (), s32[]{:S(2)}) async-start(), calls=%async_computation | async-start | bytes 131072 | tf_op jit(solution)/shard_map/while/body/eval_jaxpr/psum | solution.py:48
  744.6 34.6 %all-reduce.2.cloned.1.call-start = ((), (), s32[]{:S(2)}) async-start(), calls=%async_computation | async-start | bytes 131072 | tf_op jit(solution)/shard_map/while/body/eval_jaxpr/psum | solution.py:48
  817.9 34.2 %all-reduce.2.cloned.1.call-start = ((), (), s32[]{:S(2)}) async-start(), calls=%async_computation | async-start | bytes 131072 | tf_op jit(solution)/shard_map/while/body/eval_jaxpr/psum | solution.py:48
  891.0 34.6 %all-reduce.2.cloned.1.call-start = ((), (), s32[]{:S(2)}) async-start(), calls=%async_computation | async-start | bytes 131072 | tf_op jit(solution)/shard_map/while/body/eval_jaxpr/psum | solution.py:48
  964.4 34.2 %all-reduce.2.cloned.1.call-start = ((), (), s32[]{:S(2)}) async-start(), calls=%async_computation | async-start | bytes 131072 | tf_op jit(solution)/shard_map/while/body/eval_jaxpr/psum | solution.py:48
  1037.4 34.3 %all-reduce.2.cloned.1.call-start = ((), (), s32[]{:S(2)}) async-start(), calls=%async_computation | async-start | bytes 131072 | tf_op jit(solution)/shard_map/while/body/eval_jaxpr/psum | solution.py:48
  1110.5 34.2 %all-reduce.2.cloned.1.call-start = ((), (), s32[]{:S(2)}) async-start(), calls=%async_computation | async-start | bytes 131072 | tf_op jit(solution)/shard_map/while/body/eval_jaxpr/psum | solution.py:48
  1183.5 0.7 copy-start.1
Sparse Core Ops, SparseCore 0:
  12.4 34.2 all-reduce.1
  88.6 31.4 all-reduce.1
  162.0 31.3 all-reduce.1
  235.0 31.3 all-reduce.1
  308.1 31.3 all-reduce.1
  381.1 31.3 all-reduce.1
  454.5 31.4 all-reduce.1
  527.8 31.4 all-reduce.1
  601.2 31.4 all-reduce.1
  674.3 31.4 all-reduce.1
  747.7 31.4 all-reduce.1
  820.7 31.3 all-reduce.1
  894.1 31.4 all-reduce.1
  967.2 31.3 all-reduce.1
  1040.2 31.3 all-reduce.1
  1113.3 31.3 all-reduce.1
